TPU v7x, 32 devices: a whole 2x2x4 slice. The times are simulated.
32 devices in a mesh: gx: 8 (over y, x, core), gy: 4 (over z).
Axes of the slice: x: 2, y: 2, z: 4, core: 2. Of those that a mesh axis runs over, the one named last changes fastest.
Arguments:
- field: float32 [65536, 512], P(('gx', 'gy')), may hold values from -6 to 6
Outputs:
- spectrum: float32 [65536, 512], P('gx', 'gy')
All inputs are finite; a program needn't handle non-finite values.
Results may differ from a plain program's by a relative error of at most 0.00007.
Values sent between devices are 32-bit elements; how exact they have to be, the bound alone decides.
A program may use at most 64 MiB of HBM per device.

v0:
```python
import math
import jax
import jax.numpy as jnp
from jax import lax
from jax.sharding import PartitionSpec as P

P_SIZE = 256
Q = 256
highest = lax.Precision.HIGHEST


def mat_dot(left, right):
    return jnp.dot(left, right, precision=highest, preferred_element_type=jnp.float32)


def finish(spec_real, spec_imag, frequency):
    length = P_SIZE * Q
    phases = math.pi / (2.0 * length) * frequency.astype(jnp.float32)
    factor = math.sqrt(2.0 / length)
    return factor * (
        jnp.cos(phases)[:, :, None] * spec_real + jnp.sin(phases)[:, :, None] * spec_imag
    )


def body(field):
    groups = lax.axis_size("gx")
    position = lax.axis_index("gx")
    length = P_SIZE * Q
    joined = lax.all_to_all(field, "gy", split_axis=1, concat_axis=0, tiled=True)
    row_count = joined.shape[0]
    col_width = joined.shape[1]
    half_rows = P_SIZE // (2 * groups)
    local_q = Q // groups
    local_p = P_SIZE // groups
    paired = joined.reshape(row_count // 2, 2, col_width)
    even_rows = paired[:, 0].reshape(half_rows, Q, col_width)
    odd_rows = jnp.flip(paired[:, 1].reshape(half_rows, Q, col_width), axis=1)
    low_half, high_half = (
        lax.all_to_all(even_rows, "gx", split_axis=1, concat_axis=0, tiled=True),
        lax.all_to_all(odd_rows, "gx", split_axis=1, concat_axis=0, tiled=True),
    )
    freq_first = jnp.arange(P_SIZE, dtype=jnp.int32)
    place_low = jnp.arange(P_SIZE // 2, dtype=jnp.int32)
    place_high = P_SIZE - 1 - place_low
    two_pi = 2.0 * math.pi
    low_phase = (
        two_pi / P_SIZE * (freq_first[:, None] * place_low[None, :] % P_SIZE).astype(jnp.float32)
    )
    high_phase = (
        two_pi / P_SIZE * (freq_first[:, None] * place_high[None, :] % P_SIZE).astype(jnp.float32)
    )
    flat_low = low_half.reshape(P_SIZE // 2, local_q * col_width)
    flat_high = high_half.reshape(P_SIZE // 2, local_q * col_width)
    cos_part = (
        mat_dot(jnp.cos(low_phase), flat_low) + mat_dot(jnp.cos(high_phase), flat_high)
    ).reshape(P_SIZE, local_q, col_width)
    sin_part = (
        mat_dot(jnp.sin(low_phase), flat_low) + mat_dot(jnp.sin(high_phase), flat_high)
    ).reshape(P_SIZE, local_q, col_width)
    part_imag = -sin_part
    second_place = position * local_q + jnp.arange(local_q, dtype=jnp.int32)
    turn_phase = (
        two_pi / length * (freq_first[:, None] * second_place[None, :] % length).astype(jnp.float32)
    )
    turn_cos = jnp.cos(turn_phase)[:, :, None]
    turn_sin = jnp.sin(turn_phase)[:, :, None]
    turned_real = cos_part * turn_cos + part_imag * turn_sin
    turned_imag = part_imag * turn_cos - cos_part * turn_sin
    moved_real, moved_imag = (
        lax.all_to_all(turned_real, "gx", split_axis=0, concat_axis=1, tiled=True),
        lax.all_to_all(turned_imag, "gx", split_axis=0, concat_axis=1, tiled=True),
    )
    second_index = jnp.arange(Q, dtype=jnp.int32)
    row_phase = two_pi / Q * (second_index[:, None] * second_index[None, :] % Q).astype(jnp.float32)
    row_cos = jnp.cos(row_phase)
    row_sin = jnp.sin(row_phase)
    spec_real = jnp.einsum("jb,kbc->jkc", row_cos, moved_real, precision=highest) + jnp.einsum(
        "jb,kbc->jkc", row_sin, moved_imag, precision=highest
    )
    spec_imag = jnp.einsum("jb,kbc->jkc", row_cos, moved_imag, precision=highest) - jnp.einsum(
        "jb,kbc->jkc", row_sin, moved_real, precision=highest
    )
    block_rows = lax.dynamic_slice_in_dim(freq_first, position * local_p, local_p, 0)
    frequency = block_rows[None, :] + P_SIZE * second_index[:, None]
    result = finish(spec_real, spec_imag, frequency)
    arrived = lax.all_to_all(result, "gx", split_axis=0, concat_axis=1, tiled=True)
    return arrived.reshape(local_q * P_SIZE, col_width)


def solution(mesh):
    in_specs = (P(("gx", "gy"), None),)
    out_specs = P("gx", "gy")
    return jax.shard_map(body, mesh=mesh, in_specs=in_specs, out_specs=out_specs, check_vma=False)
```

profile of v0, /device:TPU:0, one launch (start us, length us, event | category | flops | bytes accessed | tf_op | source)
XLA Modules:
  0.0 380.9 jit_solution(13258083812697321297)
XLA Ops:
  0.0 5.3 %copy.15 = f32[2048,512]{0,1:T(8,128)} copy(f32[2048,512]{1,0:T(8,128)} %param.1) | data formatting | bytes 8388608 | tf_op args[0]
  5.3 100.6 %all_to_all.97 = f32[2048,4,128]{0,2,1:T(8,128)} all-to-all(f32[2048,4,128]{0,2,1:T(8,128)} %bitcast.81), channel_id=1, replica_groups=mesh['gx'=8,'gy'=4] {'gy'}, dimensions={1} | all-to-all | bytes 8388608 | tf_op jit(solution)/shard_map/all_to_all | solution.py:29
  105.9 5.3 %copy.16 = f32[4,2048,128]{2,1,0:T(8,128)} copy(f32[4,2048,128]{1,2,0:T(8,128)} %bitcast.79) | data formatting | bytes 8388608 | tf_op jit(solution)/shard_map/all_to_all | solution.py:29
  111.2 7.7 %fusion.96 = (f32[4096,1,128]{2,1,0:T(1,128)}, f32[4096,1,128]{2,1,0:T(1,128)S(1)}) fusion(f32[4096,2,128]{2,1,0:T(2,128)} %bitcast.78), kind=kLoop, calls=%fused_computation.111 | loop fusion | bytes 8388608 | tf_op jit(solution)/shard_map/slice | solution.py:37
  118.9 2.5 copy.17
  121.4 3.8 all-to-all-start.1
  125.2 4.1 %copy.20 = f32[16,256,128]{2,0,1:T(8,128)} copy(f32[16,256,128]{2,1,0:T(8,128)} %bitcast.83) | data formatting | bytes 4194304 | tf_op jit(solution)/shard_map/reshape;squeeze | solution.py:37
  129.3 3.1 rev.4
  132.4 19.4 %all-to-all-done.1 = f32[16,256,128]{2,0,1:T(8,128)S(1)} async-done(((f32[16,256,128]{2,0,1:T(8,128)}), f32[16,256,128]{2,0,1:T(8,128)S(1)}, u32[]{:S(2)}, u32[]{:S(2)}) %all-to-all-start.1) | async-done | bytes 2097184 | tf_op jit(solution)/shard_map/all_to_all | solution.py:39
  151.8 4.9 %all-to-all-start.2 = ((f32[16,256,128]{2,0,1:T(8,128)}), f32[16,256,128]{2,0,1:T(8,128)}, u32[]{:S(2)}, u32[]{:S(2)}) async-start(f32[16,256,128]{2,0,1:T(8,128)} %rev.4), calls=%async_computation.2 | async-start | bytes 4194304 | tf_op jit(solution)/shard_map/all_to_all | solution.py:40
  156.7 0.5 fusion.57
  157.3 0.6 copy.19
  157.9 7.3 %fusion.9 = f32[256,4096]{1,0:T(8,128)} fusion(f32[16,8,32,128]{3,2,1,0:T(8,128)S(1)} %bitcast.73), kind=kOutput, calls=%fused_computation.16 | convolution fusion | flops 1611071488 | bytes 6291456 | tf_op jit(solution)/shard_map/dot_general | solution.py:13
  165.2 7.5 %fusion.7 = f32[256,4096]{1,0:T(8,128)} fusion(f32[16,8,32,128]{3,2,1,0:T(8,128)S(1)} %bitcast.74), kind=kOutput, calls=%fused_computation.14 | convolution fusion | flops 1611071488 | bytes 6291456 | tf_op jit(solution)/shard_map/dot_general | solution.py:13
  172.7 10.6 %all-to-all-done.2 = f32[16,256,128]{2,0,1:T(8,128)} async-done(((f32[16,256,128]{2,0,1:T(8,128)}), f32[16,256,128]{2,0,1:T(8,128)}, u32[]{:S(2)}, u32[]{:S(2)}) %all-to-all-start.2) | async-done | bytes 2097184 | tf_op jit(solution)/shard_map/all_to_all | solution.py:40
  183.3 0.0 copy-start.3
  183.3 2.4 copy.22
  185.7 0.4 copy-done.3
  186.1 4.9 %fusion.3 = f32[32,8,32,128]{3,1,2,0:T(8,128)S(1)} fusion(f32[256,4096]{1,0:T(8,128)S(1)} %copy-done.3, f32[16,8,32,128]{3,2,1,0:T(8,128)S(1)} %bitcast.75, s32[128]{0:T(128)S(1)} %iota_subtract_fusion), kind=kOutput, calls=%fused_computation.10 | convolution fusion | flops 1612120064 | bytes 10486272 | tf_op jit(solution)/shard_map/dot_general | solution.py:13
  191.1 0.0 copy-start.2
  191.1 0.8 copy.31
  191.9 1.4 copy-done.2
  193.3 5.0 %fusion.4 = f32[32,8,32,128]{3,1,2,0:T(8,128)S(1)} fusion(f32[256,4096]{1,0:T(8,128)S(1)} %copy-done.2, f32[16,8,32,128]{3,2,1,0:T(8,128)S(1)} %bitcast.76, s32[128]{0:T(128)S(1)} %iota_subtract_fusion), kind=kOutput, calls=%fused_computation.11 | convolution fusion | flops 1613168640 | bytes 10486272 | tf_op jit(solution)/shard_map/dot_general | solution.py:13
  198.2 1.0 copy.32
  199.2 4.6 %fusion.1 = (f32[256,32,128]{2,1,0:T(8,128)}, f32[256,32,128]{2,1,0:T(8,128)S(1)}) fusion(f32[32,8,32,128]{3,2,1,0:T(8,128)S(1)} %copy.32, f32[32,8,32,128]{3,2,1,0:T(8,128)S(1)} %copy.31, f32[256,32]{1,0:T(8,128)S(1)} %get-tuple-element.12, f32[256,32]{1,0:T(8,128)S(1)} %get-tuple-element.11), kind=kLoop, calls=%fused_computation.5 | loop fusion | flops 6291456 | bytes 16842752 | tf_op jit(solution)/shard_map/add | solution.py:67
  203.8 52.3 %all_to_all.98 = f32[256,32,128]{2,1,0:T(8,128)} all-to-all(f32[256,32,128]{2,1,0:T(8,128)S(1)} %get-tuple-element.6), channel_id=1, replica_groups=mesh['gx'=8,'gy'=4] {'gx'}, dimensions={0} | all-to-all | bytes 8388608 | tf_op jit(solution)/shard_map/all_to_all | solution.py:71
  256.1 4.6 %all-to-all-start.3 = ((f32[256,32,128]{2,1,0:T(8,128)}), f32[256,32,128]{2,1,0:T(8,128)}, u32[]{:S(2)}, u32[]{:S(2)}) async-start(f32[256,32,128]{2,1,0:T(8,128)} %get-tuple-element.5), calls=%async_computation.3 | async-start | bytes 8388608 | tf_op jit(solution)/shard_map/all_to_all | solution.py:70
  260.7 0.1 dynamic_slice.3
  260.8 0.2 fusion.63
  261.0 2.8 copy.24
  263.8 7.1 %fusion.19 = f32[256,32,128]{2,0,1:T(8,128)} fusion(f32[32,256,128]{2,1,0:T(8,128)S(1)} %bitcast.71), kind=kOutput, calls=%fused_computation.29 | convolution fusion | flops 3222142976 | bytes 8388608 | tf_op jit(solution)/shard_map/jb,kbc->jkc/dot_general | solution.py:77
  270.9 7.3 %fusion.21 = f32[256,32,128]{2,0,1:T(8,128)} fusion(f32[32,256,128]{2,1,0:T(8,128)S(1)} %bitcast.72), kind=kOutput, calls=%fused_computation.31 | convolution fusion | flops 3222142976 | bytes 8388608 | tf_op jit(solution)/shard_map/jb,kbc->jkc/dot_general | solution.py:80
  278.2 31.5 %all-to-all-done.3 = f32[256,32,128]{2,1,0:T(8,128)} async-done(((f32[256,32,128]{2,1,0:T(8,128)}), f32[256,32,128]{2,1,0:T(8,128)}, u32[]{:S(2)}, u32[]{:S(2)}) %all-to-all-start.3) | async-done | bytes 4194336 | tf_op jit(solution)/shard_map/all_to_all | solution.py:70
  309.8 2.8 copy.23
  312.6 0.0 copy-start
  312.6 0.0 copy-start.1
  312.6 4.8 %fusion.23 = f32[256,32,128]{2,0,1:T(8,128)S(1)} fusion(f32[32,256,128]{2,1,0:T(8,128)S(1)} %bitcast.69), kind=kOutput, calls=%fused_computation.33 | convolution fusion | flops 3222142976 | bytes 8388608 | tf_op jit(solution)/shard_map/jb,kbc->jkc/dot_general | solution.py:77
  317.4 0.0 copy-done
  317.4 0.0 copy-done.1
  317.4 6.1 %add_multiply_fusion = f32[256,32,128]{2,0,1:T(8,128)S(1)} fusion(f32[256,32,128]{2,0,1:T(8,128)S(1)} %copy-done.1, f32[256,32,128]{2,0,1:T(8,128)S(1)} %fusion.23, f32[256,32,128]{2,0,1:T(8,128)S(1)} %copy-done, f32[32,256,128]{2,1,0:T(8,128)S(1)} %bitcast.70, f32[256,32]{0,1:T(8,128)S(1)} %get-tuple-element.10, f32[256,32]{0,1:T(8,128)S(1)} %get-tuple-element.9), kind=kOutput, calls=%fused_computation.9 | convolution fusion | flops 3228434432 | bytes 21037056 | tf_op jit(solution)/shard_map/jb,kbc->jkc/dot_general | solution.py:80
  323.5 2.7 copy.25
  326.3 51.5 %all_to_all.99 = f32[256,32,128]{2,1,0:T(8,128)S(1)} all-to-all(f32[256,32,128]{2,1,0:T(8,128)S(1)} %copy.25), channel_id=1, replica_groups=mesh['gx'=8,'gy'=4] {'gx'}, dimensions={0} | all-to-all | bytes 8388608 | tf_op jit(solution)/shard_map/all_to_all | solution.py:86
  377.8 2.7 copy.26
  (4 shorter events, 0.0 us)
Async XLA Ops:
  121.4 30.4 %all-to-all-start.1 = ((f32[16,256,128]{2,0,1:T(8,128)}), f32[16,256,128]{2,0,1:T(8,128)S(1)}, u32[]{:S(2)}, u32[]{:S(2)}) async-start(f32[16,256,128]{2,0,1:T(8,128)} %copy.17), calls=%async_computation.1 | async-start | bytes 4194304 | tf_op jit(solution)/shard_map/all_to_all | solution.py:39
  151.8 31.5 %all-to-all-start.2 = ((f32[16,256,128]{2,0,1:T(8,128)}), f32[16,256,128]{2,0,1:T(8,128)}, u32[]{:S(2)}, u32[]{:S(2)}) async-start(f32[16,256,128]{2,0,1:T(8,128)} %rev.4), calls=%async_computation.2 | async-start | bytes 4194304 | tf_op jit(solution)/shard_map/all_to_all | solution.py:40
  183.3 2.8 copy-start.3
  191.1 2.2 copy-start.2
  256.1 53.7 %all-to-all-start.3 = ((f32[256,32,128]{2,1,0:T(8,128)}), f32[256,32,128]{2,1,0:T(8,128)}, u32[]{:S(2)}, u32[]{:S(2)}) async-start(f32[256,32,128]{2,1,0:T(8,128)} %get-tuple-element.5), calls=%async_computation.3 | async-start | bytes 8388608 | tf_op jit(solution)/shard_map/all_to_all | solution.py:70
  312.6 4.8 %copy-start = (f32[256,32,128]{2,0,1:T(8,128)S(1)}, f32[256,32,128]{2,0,1:T(8,128)}, u32[]{:S(2)}) copy-start(f32[256,32,128]{2,0,1:T(8,128)} %fusion.19) | copy-start | bytes 12582916
  312.6 4.8 %copy-start.1 = (f32[256,32,128]{2,0,1:T(8,128)S(1)}, f32[256,32,128]{2,0,1:T(8,128)}, u32[]{:S(2)}) copy-start(f32[256,32,128]{2,0,1:T(8,128)} %fusion.21) | copy-start | bytes 12582916
where the time goes:
time: 386 us; the launch traced here: 381 us
  blocking collectives  204 us (53%)
  waiting for transfers between devices  61.6 us (16%)
  matrix products  50 us (13%)
  local copies, waits for them, and re-layouts  45.8 us (12%)
  starting transfers between devices  13.2 us (3%)
  other arithmetic  5.36 us (1%)
    all_to_all x1, blocking collectives, body(): lax.all_to_all(field, 'gy', split_axis=1, concat_axis=0, tiled=True)  101 us
    all_to_all x1, blocking collectives, body(): lax.all_to_all(turned_imag, 'gx', split_axis=0, concat_axis=1, tiled=True)  52.3 us
    all_to_all x1, blocking collectives, body(): lax.all_to_all(result, 'gx', split_axis=0, concat_axis=1, tiled=True)  51.5 us
    all_to_all x1, waiting for transfers between devices, body(): lax.all_to_all(turned_real, 'gx', split_axis=0, concat_axis=1, tiled=True)  31.5 us
    dot_general x4, matrix products, mat_dot(): jnp.dot(left, right, precision=highest, preferred_element_type=jnp.float32)  24.7 us
    all_to_all x1, waiting for transfers between devices, body(): lax.all_to_all(even_rows, 'gx', split_axis=1, concat_axis=0, tiled=True)  19.4 us
    all_to_all x1, waiting for transfers between devices, body(): lax.all_to_all(odd_rows, 'gx', split_axis=1, concat_axis=0, tiled=True)  10.6 us
    unnamed x11, local copies, waits for them, and re-layouts  8.93 us
  transfers between devices with their start and end apart: 3, of which 3 were waited for; matrix products, arithmetic and copies ran while one was open for 11% of the time, Pallas kernels for 0%

commit v1 on v0

--- a/solution.py
+++ b/solution.py
@@ -68,7 +68,12 @@
     turned_imag = part_imag * turn_cos - cos_part * turn_sin
     moved_real, moved_imag = (
         lax.all_to_all(turned_real, "gx", split_axis=0, concat_axis=1, tiled=True),
-        lax.all_to_all(turned_imag, "gx", split_axis=0, concat_axis=1, tiled=True),
+        jnp.concatenate(
+            lax.all_to_all(
+                jnp.stack(jnp.split(turned_imag, lax.axis_size("gx"), axis=0)), "gx", 0, 0
+            ),
+            axis=1,
+        ),
     )
     second_index = jnp.arange(Q, dtype=jnp.int32)
     row_phase = two_pi / Q * (second_index[:, None] * second_index[None, :] % Q).astype(jnp.float32)

time: 386 us -> 386 us (level)
    unnamed x11 -> x18, local copies, waits for them, and re-layouts: 8.93 us -> 9.19 us
where the time goes in v1:
time: 386 us; the launch traced here: 381 us
  blocking collectives  204 us (53%)
  waiting for transfers between devices  61.6 us (16%)
  matrix products  50 us (13%)
  local copies, waits for them, and re-layouts  46.1 us (12%)
  starting transfers between devices  13.2 us (3%)
  other arithmetic  5.35 us (1%)
    all_to_all x1, blocking collectives, body(): lax.all_to_all(field, 'gy', split_axis=1, concat_axis=0, tiled=True)  101 us
    all_to_all x1, blocking collectives, body(): lax.all_to_all(jnp.stack(jnp.split(turned_imag, lax.axis_size('gx'), axis...  52.3 us
    all_to_all x1, blocking collectives, body(): lax.all_to_all(result, 'gx', split_axis=0, concat_axis=1, tiled=True)  51.5 us
    all_to_all x1, waiting for transfers between devices, body(): lax.all_to_all(turned_real, 'gx', split_axis=0, concat_axis=1, tiled=True)  31.5 us
    dot_general x4, matrix products, mat_dot(): jnp.dot(left, right, precision=highest, preferred_element_type=jnp.float32)  24.7 us
    all_to_all x1, waiting for transfers between devices, body(): lax.all_to_all(even_rows, 'gx', split_axis=1, concat_axis=0, tiled=True)  19.4 us
    all_to_all x1, waiting for transfers between devices, body(): lax.all_to_all(odd_rows, 'gx', split_axis=1, concat_axis=0, tiled=True)  10.6 us
    unnamed x18, local copies, waits for them, and re-layouts  9.19 us
  transfers between devices with their start and end apart: 3, of which 3 were waited for; matrix products, arithmetic and copies ran while one was open for 11% of the time, Pallas kernels for 0%

profile of v1, /device:TPU:0, one launch (start us, length us, event | category | flops | bytes accessed | tf_op | source)
XLA Modules:
  0.0 381.3 jit_solution(16232786728314117846)
XLA Ops:
  0.0 5.3 %copy.15 = f32[2048,512]{0,1:T(8,128)} copy(f32[2048,512]{1,0:T(8,128)} %param.1) | data formatting | bytes 8388608 | tf_op args[0]
  5.3 100.6 %all_to_all.84 = f32[2048,4,128]{0,2,1:T(8,128)} all-to-all(f32[2048,4,128]{0,2,1:T(8,128)} %bitcast.111), channel_id=1, replica_groups=mesh['gx'=8,'gy'=4] {'gy'}, dimensions={1} | all-to-all | bytes 8388608 | tf_op jit(solution)/shard_map/all_to_all | solution.py:29
  105.9 5.3 %copy.16 = f32[4,2048,128]{2,1,0:T(8,128)} copy(f32[4,2048,128]{1,2,0:T(8,128)} %bitcast.109) | data formatting | bytes 8388608 | tf_op jit(solution)/shard_map/all_to_all | solution.py:29
  111.2 7.7 %fusion.104 = (f32[4096,1,128]{2,1,0:T(1,128)}, f32[4096,1,128]{2,1,0:T(1,128)S(1)}) fusion(f32[4096,2,128]{2,1,0:T(2,128)} %bitcast.108), kind=kLoop, calls=%fused_computation.127 | loop fusion | bytes 8388608 | tf_op jit(solution)/shard_map/slice | solution.py:37
  118.9 2.5 copy.17
  121.4 3.8 all-to-all-start.1
  125.2 4.1 %copy.20 = f32[16,256,128]{2,0,1:T(8,128)} copy(f32[16,256,128]{2,1,0:T(8,128)} %bitcast.113) | data formatting | bytes 4194304 | tf_op jit(solution)/shard_map/reshape;squeeze | solution.py:37
  129.3 3.1 rev.4
  132.4 19.4 %all-to-all-done.1 = f32[16,256,128]{2,0,1:T(8,128)S(1)} async-done(((f32[16,256,128]{2,0,1:T(8,128)}), f32[16,256,128]{2,0,1:T(8,128)S(1)}, u32[]{:S(2)}, u32[]{:S(2)}) %all-to-all-start.1) | async-done | bytes 2097184 | tf_op jit(solution)/shard_map/all_to_all | solution.py:39
  151.8 4.9 %all-to-all-start.2 = ((f32[16,256,128]{2,0,1:T(8,128)}), f32[16,256,128]{2,0,1:T(8,128)}, u32[]{:S(2)}, u32[]{:S(2)}) async-start(f32[16,256,128]{2,0,1:T(8,128)} %rev.4), calls=%async_computation.2 | async-start | bytes 4194304 | tf_op jit(solution)/shard_map/all_to_all | solution.py:40
  156.7 0.5 fusion.65
  157.3 0.6 copy.19
  157.9 7.3 %fusion.9 = f32[256,4096]{1,0:T(8,128)} fusion(f32[16,8,32,128]{3,2,1,0:T(8,128)S(1)} %bitcast.103), kind=kOutput, calls=%fused_computation.16 | convolution fusion | flops 1611071488 | bytes 6291456 | tf_op jit(solution)/shard_map/dot_general | solution.py:13
  165.2 7.5 %fusion.7 = f32[256,4096]{1,0:T(8,128)} fusion(f32[16,8,32,128]{3,2,1,0:T(8,128)S(1)} %bitcast.104), kind=kOutput, calls=%fused_computation.14 | convolution fusion | flops 1611071488 | bytes 6291456 | tf_op jit(solution)/shard_map/dot_general | solution.py:13
  172.7 10.6 %all-to-all-done.2 = f32[16,256,128]{2,0,1:T(8,128)} async-done(((f32[16,256,128]{2,0,1:T(8,128)}), f32[16,256,128]{2,0,1:T(8,128)}, u32[]{:S(2)}, u32[]{:S(2)}) %all-to-all-start.2) | async-done | bytes 2097184 | tf_op jit(solution)/shard_map/all_to_all | solution.py:40
  183.3 0.0 copy-start.3
  183.3 2.4 copy.22
  185.7 0.4 copy-done.3
  186.1 4.9 %fusion.3 = f32[32,8,32,128]{3,1,2,0:T(8,128)S(1)} fusion(f32[256,4096]{1,0:T(8,128)S(1)} %copy-done.3, f32[16,8,32,128]{3,2,1,0:T(8,128)S(1)} %bitcast.105, s32[128]{0:T(128)S(1)} %iota_subtract_fusion), kind=kOutput, calls=%fused_computation.10 | convolution fusion | flops 1612120064 | bytes 10486272 | tf_op jit(solution)/shard_map/dot_general | solution.py:13
  191.1 0.0 copy-start.2
  191.1 0.8 copy.31
  191.9 1.4 copy-done.2
  193.3 5.0 %fusion.4 = f32[32,8,32,128]{3,1,2,0:T(8,128)S(1)} fusion(f32[256,4096]{1,0:T(8,128)S(1)} %copy-done.2, f32[16,8,32,128]{3,2,1,0:T(8,128)S(1)} %bitcast.106, s32[128]{0:T(128)S(1)} %iota_subtract_fusion), kind=kOutput, calls=%fused_computation.11 | convolution fusion | flops 1613168640 | bytes 10486272 | tf_op jit(solution)/shard_map/dot_general | solution.py:13
  198.2 1.0 copy.32
  199.2 4.6 %fusion.1 = (f32[256,32,128]{2,1,0:T(8,128)}, f32[256,32,128]{2,1,0:T(8,128)S(1)}) fusion(f32[32,8,32,128]{3,2,1,0:T(8,128)S(1)} %copy.32, f32[32,8,32,128]{3,2,1,0:T(8,128)S(1)} %copy.31, f32[256,32]{1,0:T(8,128)S(1)} %get-tuple-element.12, f32[256,32]{1,0:T(8,128)S(1)} %get-tuple-element.11), kind=kLoop, calls=%fused_computation.5 | loop fusion | flops 6291456 | bytes 16842752 | tf_op jit(solution)/shard_map/add | solution.py:67
  204.2 52.3 %all_to_all.85 = f32[8,32,32,128]{3,2,1,0:T(8,128)} all-to-all(f32[8,32,32,128]{3,2,1,0:T(8,128)S(1)} %fusion.15), channel_id=1, replica_groups=mesh['gx'=8,'gy'=4] {'gx'}, dimensions={0} | all-to-all | bytes 8388608 | tf_op jit(solution)/shard_map/all_to_all | solution.py:72
  256.5 4.6 %all-to-all-start.3 = ((f32[256,32,128]{2,1,0:T(8,128)}), f32[256,32,128]{2,1,0:T(8,128)}, u32[]{:S(2)}, u32[]{:S(2)}) async-start(f32[256,32,128]{2,1,0:T(8,128)} %get-tuple-element.5), calls=%async_computation.3 | async-start | bytes 8388608 | tf_op jit(solution)/shard_map/all_to_all | solution.py:70
  261.0 0.1 dynamic_slice.3
  261.1 0.2 fusion.71
  261.3 2.8 copy.24
  264.2 7.1 %fusion.27 = f32[256,32,128]{2,0,1:T(8,128)} fusion(f32[32,256,128]{2,1,0:T(8,128)S(1)} %bitcast.101), kind=kOutput, calls=%fused_computation.45 | convolution fusion | flops 3222142976 | bytes 8388608 | tf_op jit(solution)/shard_map/jb,kbc->jkc/dot_general | solution.py:82
  271.3 7.3 %fusion.29 = f32[256,32,128]{2,0,1:T(8,128)} fusion(f32[32,256,128]{2,1,0:T(8,128)S(1)} %bitcast.102), kind=kOutput, calls=%fused_computation.47 | convolution fusion | flops 3222142976 | bytes 8388608 | tf_op jit(solution)/shard_map/jb,kbc->jkc/dot_general | solution.py:85
  278.6 31.5 %all-to-all-done.3 = f32[256,32,128]{2,1,0:T(8,128)} async-done(((f32[256,32,128]{2,1,0:T(8,128)}), f32[256,32,128]{2,1,0:T(8,128)}, u32[]{:S(2)}, u32[]{:S(2)}) %all-to-all-start.3) | async-done | bytes 4194336 | tf_op jit(solution)/shard_map/all_to_all | solution.py:70
  310.1 2.8 copy.23
  313.0 0.0 copy-start
  313.0 0.0 copy-start.1
  313.0 4.8 %fusion.31 = f32[256,32,128]{2,0,1:T(8,128)S(1)} fusion(f32[32,256,128]{2,1,0:T(8,128)S(1)} %bitcast.99), kind=kOutput, calls=%fused_computation.49 | convolution fusion | flops 3222142976 | bytes 8388608 | tf_op jit(solution)/shard_map/jb,kbc->jkc/dot_general | solution.py:82
  317.7 0.0 copy-done
  317.8 0.0 copy-done.1
  317.8 6.1 %add_multiply_fusion = f32[256,32,128]{2,0,1:T(8,128)S(1)} fusion(f32[256,32,128]{2,0,1:T(8,128)S(1)} %copy-done.1, f32[256,32,128]{2,0,1:T(8,128)S(1)} %fusion.31, f32[256,32,128]{2,0,1:T(8,128)S(1)} %copy-done, f32[32,256,128]{2,1,0:T(8,128)S(1)} %bitcast.100, f32[256,32]{0,1:T(8,128)S(1)} %get-tuple-element.10, f32[256,32]{0,1:T(8,128)S(1)} %get-tuple-element.9), kind=kOutput, calls=%fused_computation.9 | convolution fusion | flops 3228434432 | bytes 21037056 | tf_op jit(solution)/shard_map/jb,kbc->jkc/dot_general | solution.py:85
  323.9 2.7 copy.25
  326.6 51.5 %all_to_all.86 = f32[256,32,128]{2,1,0:T(8,128)S(1)} all-to-all(f32[256,32,128]{2,1,0:T(8,128)S(1)} %copy.25), channel_id=1, replica_groups=mesh['gx'=8,'gy'=4] {'gx'}, dimensions={0} | all-to-all | bytes 8388608 | tf_op jit(solution)/shard_map/all_to_all | solution.py:91
  378.1 2.7 copy.26
  (12 shorter events, 0.3 us)
Async XLA Ops:
  121.4 30.4 %all-to-all-start.1 = ((f32[16,256,128]{2,0,1:T(8,128)}), f32[16,256,128]{2,0,1:T(8,128)S(1)}, u32[]{:S(2)}, u32[]{:S(2)}) async-start(f32[16,256,128]{2,0,1:T(8,128)} %copy.17), calls=%async_computation.1 | async-start | bytes 4194304 | tf_op jit(solution)/shard_map/all_to_all | solution.py:39
  151.8 31.5 %all-to-all-start.2 = ((f32[16,256,128]{2,0,1:T(8,128)}), f32[16,256,128]{2,0,1:T(8,128)}, u32[]{:S(2)}, u32[]{:S(2)}) async-start(f32[16,256,128]{2,0,1:T(8,128)} %rev.4), calls=%async_computation.2 | async-start | bytes 4194304 | tf_op jit(solution)/shard_map/all_to_all | solution.py:40
  183.3 2.8 copy-start.3
  191.1 2.2 copy-start.2
  256.5 53.7 %all-to-all-start.3 = ((f32[256,32,128]{2,1,0:T(8,128)}), f32[256,32,128]{2,1,0:T(8,128)}, u32[]{:S(2)}, u32[]{:S(2)}) async-start(f32[256,32,128]{2,1,0:T(8,128)} %get-tuple-element.5), calls=%async_computation.3 | async-start | bytes 8388608 | tf_op jit(solution)/shard_map/all_to_all | solution.py:70
  313.0 4.8 %copy-start = (f32[256,32,128]{2,0,1:T(8,128)S(1)}, f32[256,32,128]{2,0,1:T(8,128)}, u32[]{:S(2)}) copy-start(f32[256,32,128]{2,0,1:T(8,128)} %fusion.27) | copy-start | bytes 12582916
  313.0 4.8 %copy-start.1 = (f32[256,32,128]{2,0,1:T(8,128)S(1)}, f32[256,32,128]{2,0,1:T(8,128)}, u32[]{:S(2)}) copy-start(f32[256,32,128]{2,0,1:T(8,128)} %fusion.29) | copy-start | bytes 12582916
